TPU v7x, 32 devices: a whole 2x2x4 slice. The times are simulated.
32 devices in a mesh: fsdp: 8 (over z, x), grp: 4 (over y, core).
Axes of the slice: x: 2, y: 2, z: 4, core: 2. Of those that a mesh axis runs over, the one named last changes fastest.
Arguments:
- gradient: bfloat16 [24, 512, 512], P('fsdp', 'grp'), may hold values from -6 to 6
- left_factor: bfloat16 [96, 512, 512], P(('fsdp', 'grp'))
- right_factor: bfloat16 [96, 512, 512], P(('fsdp', 'grp'))
- block_owner: int32 [24], replicated, may hold values from 0 to 31, as said below
Outputs:
- preconditioned: bfloat16 [24, 512, 512], P('fsdp', 'grp')
Inputs may be any that keep to these rules, and one draw needn't show every extreme that they name: block_owner[b] is a device index, fsdp index times 4 plus grp index. The 3 blocks homed at one fsdp index go to devices of 3 different fsdp indices; the devices of each fsdp index own 3 blocks in all; no device owns more than 3 blocks, and at every fsdp index one device owns exactly 3.
All inputs are finite; a program needn't handle non-finite values.
Results may differ from a plain program's by a relative error of at most 0.0049.
Values may be sent and summed in bfloat16 or wider, within the bound.
A program may use at most 64 MiB of HBM per device.

v0:
```python
import jax
import jax.numpy as jnp
from jax import lax
from jax.sharding import PartitionSpec as P


def per_device(gradient, left_factor, right_factor, block_owner):
    local_blocks = gradient.shape[0]
    piece_rows = gradient.shape[1]
    block_width = gradient.shape[2]
    slot_count = left_factor.shape[0]
    columns = lax.axis_size("fsdp")
    groups = lax.axis_size("grp")
    column = lax.axis_index("fsdp")
    owners_all = block_owner.reshape(columns, local_blocks)
    dest_column = owners_all // groups
    dest_group = owners_all % groups
    mine_column = lax.dynamic_index_in_dim(dest_column, column, 0, keepdims=False)
    column_ids = jnp.arange(columns, dtype=jnp.int32)
    matching = mine_column[None, :] == column_ids[:, None]
    pick_send = matching.astype(jnp.bfloat16)
    outgoing = jnp.einsum(
        "cj,jrd->crd", pick_send, gradient, preferred_element_type=jnp.float32
    ).astype(jnp.bfloat16)
    arrived = lax.all_to_all(
        outgoing.reshape(columns * piece_rows, block_width),
        "fsdp",
        split_axis=0,
        concat_axis=0,
        tiled=True,
    )
    arrived = arrived.reshape(columns, piece_rows, block_width)
    toward = dest_column == column
    live_source = jnp.sum(toward.astype(jnp.int32), axis=1) > 0
    target = jnp.sum(jnp.where(toward, dest_group, 0), axis=1)
    same_owner = (target[None, :] == target[:, None]) & live_source[None, :] & live_source[:, None]
    before = column_ids[None, :] < column_ids[:, None]
    rank_slot = jnp.sum((same_owner & before).astype(jnp.int32), axis=1)
    group_ids = jnp.arange(groups, dtype=jnp.int32)
    slot_ids = jnp.arange(slot_count, dtype=jnp.int32)
    routing = (
        live_source[None, None, :]
        & (target[None, None, :] == group_ids[:, None, None])
        & (rank_slot[None, None, :] == slot_ids[None, :, None])
    )
    routing = routing.astype(jnp.bfloat16)
    packed = jnp.einsum(
        "oks,srd->kord", routing, arrived, preferred_element_type=jnp.float32
    ).astype(jnp.bfloat16)
    packed = packed.reshape(slot_count, groups * piece_rows, block_width)
    blocks = lax.all_to_all(packed, "grp", split_axis=1, concat_axis=1, tiled=True)
    left_product = jnp.einsum(
        "kab,kbc->kac", left_factor, blocks, preferred_element_type=jnp.float32
    ).astype(jnp.bfloat16)
    result = jnp.einsum(
        "kab,kbc->kac", left_product, right_factor, preferred_element_type=jnp.float32
    ).astype(jnp.bfloat16)
    returned = lax.all_to_all(result, "grp", split_axis=1, concat_axis=1, tiled=True)
    returned = returned.reshape(slot_count, groups, piece_rows, block_width)
    unpacked = jnp.einsum(
        "oks,kord->srd", routing, returned, preferred_element_type=jnp.float32
    ).astype(jnp.bfloat16)
    homeward = lax.all_to_all(
        unpacked.reshape(columns * piece_rows, block_width),
        "fsdp",
        split_axis=0,
        concat_axis=0,
        tiled=True,
    )
    homeward = homeward.reshape(columns, piece_rows, block_width)
    return jnp.einsum(
        "cj,crd->jrd", pick_send, homeward, preferred_element_type=jnp.float32
    ).astype(jnp.bfloat16)


def solution(mesh):
    return jax.shard_map(
        per_device,
        mesh=mesh,
        in_specs=(
            P("fsdp", "grp", None),
            P(("fsdp", "grp"), None, None),
            P(("fsdp", "grp"), None, None),
            P(),
        ),
        out_specs=P("fsdp", "grp", None),
        check_vma=False,
    )
```

profile of v0, /device:TPU:0, one launch (start us, length us, event | category | flops | bytes accessed | tf_op | source)
XLA Modules:
  0.0 135.2 jit_solution(5954696607277778726)
XLA Ops:
  0.0 0.0 copy-start
  0.0 0.8 reshape.94
  0.9 1.6 %convolution_convert_fusion.3 = bf16[8,128,512]{2,0,1:T(8,128)(2,1)S(1)} fusion(bf16[3,128,512]{2,1,0:T(8,128)(2,1)} %param.4, s32[3]{0:T(128)S(1)} %dynamic-slice_bitcast_fusion), kind=kOutput, calls=%fused_computation.7 | convolution fusion | flops 3670040 | bytes 1441804 | tf_op jit(solution)/shard_map/cj,jrd->crd/dot_general | solution.py:22
  2.5 1.3 copy.33
  3.8 7.3 %all-to-all-start = ((bf16[8,128,512]{2,1,0:T(8,128)(2,1)}), bf16[8,128,512]{2,1,0:T(8,128)(2,1)S(1)}, u32[]{:S(2)}, u32[]{:S(2)}) async-start(bf16[8,128,512]{2,1,0:T(8,128)(2,1)} %copy.33), calls=%async_computation | async-start | bytes 2097152 | tf_op jit(solution)/shard_map/all_to_all | solution.py:25
  11.1 0.1 convert_reduce_fusion.1
  11.2 0.2 convert_reduce_fusion
  11.4 25.4 %all-to-all-done = bf16[8,128,512]{2,1,0:T(8,128)(2,1)S(1)} async-done(((bf16[8,128,512]{2,1,0:T(8,128)(2,1)}), bf16[8,128,512]{2,1,0:T(8,128)(2,1)S(1)}, u32[]{:S(2)}, u32[]{:S(2)}) %all-to-all-start) | async-done | bytes 1048608 | tf_op jit(solution)/shard_map/all_to_all | solution.py:25
  36.8 1.0 fusion.2
  37.9 0.3 copy.35
  38.2 1.4 copy.36
  39.6 28.9 %all_to_all.22 = bf16[3,512,512]{2,0,1:T(4,128)(2,1)} all-to-all(bf16[3,512,512]{2,0,1:T(4,128)(2,1)S(1)} %copy.36), channel_id=1, replica_groups=mesh['fsdp'=8,'grp'=4] {'grp'}, dimensions={1} | all-to-all | bytes 3145728 | tf_op jit(solution)/shard_map/all_to_all | solution.py:51
  68.5 0.0 copy-done
  68.5 4.2 %convolution_convert_fusion = bf16[3,512,512]{2,1,0:T(8,128)(2,1)S(1)} fusion(bf16[3,512,512]{2,1,0:T(8,128)(2,1)S(1)} %copy-done, bf16[3,512,512]{2,1,0:T(8,128)(2,1)} %param.5, bf16[3,512,512]{2,0,1:T(4,128)(2,1)} %all_to_all.22), kind=kOutput, calls=%fused_computation.1 | convolution fusion | flops 1612185600 | bytes 6291456 | tf_op jit(solution)/shard_map/kab,kbc->kac/dot_general | solution.py:55
  72.7 1.4 copy.39
  74.0 28.1 %all_to_all.23 = bf16[3,512,512]{2,0,1:T(4,128)(2,1)S(1)} all-to-all(bf16[3,512,512]{2,0,1:T(4,128)(2,1)S(1)} %copy.39), channel_id=1, replica_groups=mesh['fsdp'=8,'grp'=4] {'grp'}, dimensions={1} | all-to-all | bytes 3145728 | tf_op jit(solution)/shard_map/all_to_all | solution.py:58
  102.2 2.2 %bitcast_convert_fusion = bf16[8,128,512]{2,0,1:T(8,128)(2,1)S(1)} fusion(bf16[3,4,128,512]{3,0,2,1:T(4,128)(2,1)S(1)} %bitcast.23, pred[3,8]{1,0:T(4,128)(4,1)S(1)} %iota_compare_fusion.1, pred[4,8]{1,0:T(4,128)(4,1)S(1)} %fusion.22), kind=kOutput, calls=%fused_computation | convolution fusion | flops 13107296 | bytes 2621496 | tf_op jit(solution)/shard_map/oks,kord->srd/dot_general | solution.py:60
  104.4 0.3 copy.42
  104.7 28.8 %all_to_all.24 = bf16[8,128,512]{2,1,0:T(8,128)(2,1)S(1)} all-to-all(bf16[8,128,512]{2,1,0:T(8,128)(2,1)S(1)} %copy.42), channel_id=1, replica_groups=mesh['fsdp'=8,'grp'=4] {'fsdp'}, dimensions={0} | all-to-all | bytes 2097152 | tf_op jit(solution)/shard_map/all_to_all | solution.py:63
  133.6 0.8 convolution_convert_fusion.4
  134.4 0.8 copy.44
  (5 shorter events, 0.0 us)
Async XLA Ops:
  0.0 68.5 %copy-start = (bf16[3,512,512]{2,1,0:T(8,128)(2,1)S(1)}, bf16[3,512,512]{2,1,0:T(8,128)(2,1)}, u32[]{:S(2)}) copy-start(bf16[3,512,512]{2,1,0:T(8,128)(2,1)} %param.6) | copy-start | bytes 4718596
  3.8 33.0 %all-to-all-start = ((bf16[8,128,512]{2,1,0:T(8,128)(2,1)}), bf16[8,128,512]{2,1,0:T(8,128)(2,1)S(1)}, u32[]{:S(2)}, u32[]{:S(2)}) async-start(bf16[8,128,512]{2,1,0:T(8,128)(2,1)} %copy.33), calls=%async_computation | async-start | bytes 2097152 | tf_op jit(solution)/shard_map/all_to_all | solution.py:25
where the time goes:
time: 136 us; the launch traced here: 135 us
  blocking collectives  85.9 us (63%)
  waiting for transfers between devices  25.4 us (19%)
  matrix products  9.85 us (7%)
  starting transfers between devices  7.28 us (5%)
  local copies, waits for them, and re-layouts  6.34 us (5%)
    all_to_all x1, blocking collectives, per_device(): lax.all_to_all(packed, 'grp', split_axis=1, concat_axis=1, tiled=True)  28.9 us
    all_to_all x1, blocking collectives, per_device(): lax.all_to_all(unpacked.reshape(columns * piece_rows, block_width), 'fsdp...  28.8 us
    all_to_all x1, blocking collectives, per_device(): lax.all_to_all(result, 'grp', split_axis=1, concat_axis=1, tiled=True)  28.1 us
    all_to_all x1, waiting for transfers between devices, per_device(): lax.all_to_all(outgoing.reshape(columns * piece_rows, block_width), 'fsdp...  25.4 us
    all_to_all x1, starting transfers between devices, per_device(): lax.all_to_all(outgoing.reshape(columns * piece_rows, block_width), 'fsdp...  7.28 us
    dot_general x1, matrix products, per_device(): jnp.einsum('kab,kbc->kac', left_product, right_factor, preferred_element_...  4.21 us
  transfers between devices with their start and end apart: 1, of which 1 were waited for; matrix products, arithmetic and copies ran while one was open for 0% of the time, Pallas kernels for 0%

commit v1 on v0

--- a/solution.py
+++ b/solution.py
@@ -1,7 +1,14 @@
+import functools
+
 import jax
 import jax.numpy as jnp
 from jax import lax
+from jax.experimental import pallas as pl
+from jax.experimental.pallas import tpu as pltpu
 from jax.sharding import PartitionSpec as P
+
+MESH = pl.DeviceIdType.MESH
+CHUNKS = 4
 
 
 def per_device(gradient, left_factor, right_factor, block_owner):
@@ -73,9 +80,234 @@
     ).astype(jnp.bfloat16)
 
 
+def preconditioner_kernel(
+    columns, groups, blocks, rows, width, chunks,
+    owner_ref, g_hbm, l_hbm, r_hbm, out_ref,
+    gv, lv, rv, snd, gf, lp, pc, rcvc, sely, rcvy, snd2, *rest,
+):
+    arr = rest[:chunks]
+    res = rest[chunks:2 * chunks]
+    arr2 = rest[2 * chunks:3 * chunks]
+    (load_sem, fs_s, fs_r, y_s, y_r, c_s, c_r,
+     rc_s, rc_r, ry_s, ry_r, hs_s, hs_r) = rest[3 * chunks:]
+    col = lax.axis_index("fsdp")
+    grp = lax.axis_index("grp")
+    core = grp % 2
+    half = grp // 2
+    mate = half * 2 + (1 - core)
+    across = (1 - half) * 2 + core
+    w = width // chunks
+
+    loads = [
+        pltpu.make_async_copy(g_hbm, gv, load_sem.at[0]),
+        pltpu.make_async_copy(l_hbm, lv, load_sem.at[1]),
+        pltpu.make_async_copy(r_hbm, rv, load_sem.at[2]),
+    ]
+    for load in loads:
+        load.start()
+
+    barrier = pltpu.get_barrier_semaphore()
+    for s in range(1, columns):
+        pl.semaphore_signal(barrier, inc=1, device_id={"fsdp": (col + s) % columns}, device_id_type=MESH)
+    pl.semaphore_signal(barrier, inc=1, device_id={"grp": mate}, device_id_type=MESH)
+    pl.semaphore_signal(barrier, inc=1, device_id={"grp": across}, device_id_type=MESH)
+
+    mine = [owner_ref[col * blocks + j] for j in range(blocks)]
+    my_dest = [m // groups for m in mine]
+    zero = jnp.int32(0)
+    rank_of = []
+    source = [zero] * blocks
+    count = zero
+    owner_group = zero
+    for s in range(columns):
+        rank_of.append(jnp.minimum(count, blocks - 1))
+        live = zero
+        for j in range(blocks):
+            o = owner_ref[s * blocks + j]
+            hit = (o // groups) == col
+            live = jnp.where(hit, 1, live)
+            owner_group = jnp.where(hit, o % groups, owner_group)
+        for k in range(blocks):
+            source[k] = jnp.where((live == 1) & (count == k), s, source[k])
+        count = count + live
+    owner_core = owner_group % 2
+    owner_half = owner_group // 2
+
+    def block_for(d):
+        j_d = zero
+        for j in range(1, blocks):
+            j_d = jnp.where(my_dest[j] == d, j, j_d)
+        return j_d
+
+    def rank_for(d):
+        k_d = zero
+        for s in range(columns):
+            k_d = jnp.where(d == s, rank_of[s], k_d)
+        return k_d
+
+    order = list(range(1, columns))
+    peers = {s: (col + s) % columns for s in order}
+    senders = {s: (col + columns - s) % columns for s in order}
+
+    def exchange(buf, into, q, s, send_sems, recv_sems):
+        return pltpu.make_async_remote_copy(
+            src_ref=buf.at[q, s], dst_ref=into[q].at[col],
+            send_sem=send_sems.at[q, s], recv_sem=recv_sems.at[q, s],
+            device_id={"fsdp": peers[s]}, device_id_type=MESH,
+        )
+
+    def arrival(buf, into, q, s, send_sems, recv_sems):
+        return pltpu.make_async_remote_copy(
+            src_ref=buf.at[q, s], dst_ref=into[q].at[senders[s]],
+            send_sem=send_sems.at[q, s], recv_sem=recv_sems.at[q, s],
+            device_id={"fsdp": peers[s]}, device_id_type=MESH,
+        )
+
+    def to_group(src, dst, send_sem, recv_sem, g):
+        return pltpu.make_async_remote_copy(
+            src_ref=src, dst_ref=dst, send_sem=send_sem, recv_sem=recv_sem,
+            device_id={"grp": g}, device_id_type=MESH,
+        )
+
+    loads[0].wait()
+    blocks_to = {s: block_for(peers[s]) for s in order}
+    own_block = block_for(col)
+    for q in range(chunks):
+        for s in order:
+            snd[q, s] = gv[blocks_to[s], :, q * w:(q + 1) * w]
+        arr[q][col] = gv[own_block, :, q * w:(q + 1) * w]
+    pl.semaphore_wait(barrier, columns + 1)
+    pending = []
+    for q in range(chunks):
+        for s in order:
+            c = exchange(snd, arr, q, s, fs_s, fs_r)
+            c.start()
+            pending.append(c)
+    loads[1].wait()
+    loads[2].wait()
+
+    for q in range(chunks):
+        for s in order:
+            arrival(snd, arr, q, s, fs_s, fs_r).wait_recv()
+        for k in range(blocks):
+            gf[q, grp, k] = arr[q][source[k]]
+        first = to_group(gf.at[q, grp], gf.at[q, grp], y_s.at[q], y_r.at[q], across)
+        first.start()
+        direct = to_group(gf.at[q, grp], gf.at[q, grp], c_s.at[q, 0], c_r.at[q, 0], mate)
+        direct.start()
+        to_group(gf.at[q, across], gf.at[q, across], y_s.at[q], y_r.at[q], across).wait_recv()
+        onward = to_group(gf.at[q, across], gf.at[q, across], c_s.at[q, 1], c_r.at[q, 1], mate)
+        onward.start()
+        pending += [first, direct, onward]
+        diagonal = (1 - half) * 2 + (1 - core)
+        to_group(gf.at[q, mate], gf.at[q, mate], c_s.at[q, 0], c_r.at[q, 0], mate).wait_recv()
+        to_group(gf.at[q, diagonal], gf.at[q, diagonal], c_s.at[q, 1], c_r.at[q, 1], mate).wait_recv()
+        for k in range(blocks):
+            g_cols = gf[q, :, k].reshape(groups * rows, w)
+            lp[k, :, q * w:(q + 1) * w] = jnp.dot(
+                lv[k], g_cols, preferred_element_type=jnp.float32
+            ).astype(jnp.bfloat16)
+
+    for q in range(chunks):
+        for k in range(blocks):
+            p = jnp.dot(
+                lp[k], rv[k, :, q * w:(q + 1) * w], preferred_element_type=jnp.float32
+            ).astype(jnp.bfloat16)
+            for g in range(groups):
+                pc[q, g % 2, g // 2, k] = p[g * rows:(g + 1) * rows]
+        c = to_group(pc.at[q, 1 - core], rcvc.at[q], rc_s.at[q], rc_r.at[q], mate)
+        c.start()
+        pending.append(c)
+
+    def forward_rows(q):
+        to_group(pc.at[q, 1 - core], rcvc.at[q], rc_s.at[q], rc_r.at[q], mate).wait_recv()
+        sely[q] = jnp.where(owner_core == core, pc[q, core, 1 - half], rcvc[q, 1 - half])
+        c = to_group(sely.at[q], rcvy.at[q], ry_s.at[q], ry_r.at[q], across)
+        c.start()
+        return c
+
+    for q in range(chunks):
+        pending.append(forward_rows(q))
+    ranks = {s: rank_for(peers[s]) for s in order}
+    own_rank = rank_for(col)
+    for q in range(chunks):
+        to_group(sely.at[q], rcvy.at[q], ry_s.at[q], ry_r.at[q], across).wait_recv()
+        near = jnp.where(owner_core == core, pc[q, core, half], rcvc[q, half])
+        res[q][...] = jnp.where(owner_half == half, near, rcvy[q])
+        for s in order:
+            snd2[q, s] = res[q][ranks[s]]
+            c = exchange(snd2, arr2, q, s, hs_s, hs_r)
+            c.start()
+            pending.append(c)
+        arr2[q][col] = res[q][own_rank]
+    for q in range(chunks):
+        for s in order:
+            arrival(snd2, arr2, q, s, hs_s, hs_r).wait_recv()
+        for j in range(blocks):
+            out_ref[j, :, q * w:(q + 1) * w] = arr2[q][my_dest[j]]
+    for c in pending:
+        c.wait_send()
+
+
+def per_device_fused(gradient, left_factor, right_factor, block_owner):
+    blocks, rows, width = gradient.shape
+    columns = lax.axis_size("fsdp")
+    groups = lax.axis_size("grp")
+    q = CHUNKS
+    w = width // q
+    bf = jnp.bfloat16
+    dma = pltpu.SemaphoreType.DMA
+    piece = pltpu.VMEM((columns, rows, w), bf)
+    return pl.pallas_call(
+        functools.partial(preconditioner_kernel, columns, groups, blocks, rows, width, q),
+        out_shape=jax.ShapeDtypeStruct(gradient.shape, gradient.dtype),
+        in_specs=[pl.BlockSpec(memory_space=pltpu.SMEM)] + [pl.BlockSpec(memory_space=pl.ANY)] * 3,
+        out_specs=pl.BlockSpec(memory_space=pltpu.VMEM),
+        scratch_shapes=[
+            pltpu.VMEM(gradient.shape, bf),
+            pltpu.VMEM(left_factor.shape, bf),
+            pltpu.VMEM(right_factor.shape, bf),
+            pltpu.VMEM((q, columns, rows, w), bf),
+            pltpu.VMEM((q, groups, blocks, rows, w), bf),
+            pltpu.VMEM((blocks, width, width), bf),
+            pltpu.VMEM((q, 2, 2, blocks, rows, w), bf),
+            pltpu.VMEM((q, 2, blocks, rows, w), bf),
+            pltpu.VMEM((q, blocks, rows, w), bf),
+            pltpu.VMEM((q, blocks, rows, w), bf),
+            pltpu.VMEM((q, columns, rows, w), bf),
+        ]
+        + [piece] * q
+        + [pltpu.VMEM((blocks, rows, w), bf)] * q
+        + [piece] * q
+        + [
+            dma((3,)),
+            dma((q, columns)), dma((q, columns)),
+            dma((q,)), dma((q,)),
+            dma((q, 2)), dma((q, 2)),
+            dma((q,)), dma((q,)),
+            dma((q,)), dma((q,)),
+            dma((q, columns)), dma((q, columns)),
+        ],
+        compiler_params=pltpu.CompilerParams(
+            collective_id=0, has_side_effects=True, vmem_limit_bytes=48 * 1024 * 1024
+        ),
+    )(block_owner, gradient, left_factor, right_factor)
+
+
+def per_device_any(gradient, left_factor, right_factor, block_owner):
+    blocks = gradient.shape[0]
+    fits = (
+        blocks == left_factor.shape[0]
+        and lax.axis_size("grp") == 4
+        and gradient.shape[2] % (CHUNKS * 128) == 0
+    )
+    body = per_device_fused if fits else per_device
+    return body(gradient, left_factor, right_factor, block_owner)
+
+
 def solution(mesh):
     return jax.shard_map(
-        per_device,
+        per_device_any,
         mesh=mesh,
         in_specs=(
             P("fsdp", "grp", None),

time: 136 us -> 76.5 us (0.56)
  blocking collectives: 85.9 us -> 0 us
  Pallas kernels: 0 us -> 71 us
  waiting for transfers between devices: 25.4 us -> 0 us
  matrix products: 9.85 us -> 0 us
  starting transfers between devices: 7.28 us -> 0 us
    all_to_all x3 -> x0, blocking collectives: 85.9 us -> none  [the longest x1 28.9 us: per_device(): lax.all_to_all(packed, 'grp', split_axis=1, concat_axis=1, tiled=True)]
    pallas_call x0 -> x1, Pallas kernels: none -> 71 us  [per_device_fused(): pl.pallas_call(functools.partial(preconditioner_kernel, columns, groups,...]
    all_to_all x1 -> x0, waiting for transfers between devices: 25.4 us -> none  [per_device(): lax.all_to_all(outgoing.reshape(columns * piece_rows, block_width), 'fsdp...]
    dot_general x5 -> x0, matrix products: 9.85 us -> none  [the longest x1 4.21 us: per_device(): jnp.einsum('kab,kbc->kac', left_product, right_factor, preferred_element_...]
    all_to_all x1 -> x0, starting transfers between devices: 7.28 us -> none  [per_device(): lax.all_to_all(outgoing.reshape(columns * piece_rows, block_width), 'fsdp...]
    unnamed x2 -> x9, local copies, waits for them, and re-layouts: 0.01 us -> 5.21 us
    convert_element_type x5 -> x0, local copies, waits for them, and re-layouts: 4.12 us -> none  [the longest x1 1.35 us: per_device(): result = jnp.einsum('kab,kbc->kac', left_product, right_factor, preferred...]
    reshape x2 -> x0, local copies, waits for them, and re-layouts: 2.2 us -> none  [the longest x1 1.35 us: per_device(): packed = packed.reshape(slot_count, groups * piece_rows, block_width)]
  transfers between devices with their start and end apart: 1 -> 0, of which waited for: 1 -> 0; matrix products, arithmetic and copies ran while one was open for 0% -> 0% of each run, Pallas kernels for 0% -> 0%
where the time goes in v1:
time: 76.5 us; the launch traced here: 76.2 us
  Pallas kernels  71 us (93%)
  local copies, waits for them, and re-layouts  5.21 us (7%)
    pallas_call x1, Pallas kernels, per_device_fused(): pl.pallas_call(functools.partial(preconditioner_kernel, columns, groups,...  71 us
    unnamed x9, local copies, waits for them, and re-layouts  5.21 us

profile of v1, /device:TPU:0, one launch (start us, length us, event | category | flops | bytes accessed | tf_op | source)
XLA Modules:
  0.0 76.2 jit_solution(6578620114737267358)
XLA Ops:
  0.0 0.0 copy-start
  0.0 1.4 %copy-done = bf16[3,512,512]{2,1,0:T(8,128)(2,1)S(1)} copy-done((bf16[3,512,512]{2,1,0:T(8,128)(2,1)S(1)}, bf16[3,512,512]{2,1,0:T(8,128)(2,1)}, u32[]{:S(2)}) %copy-start) | copy-done | bytes 1572888
  1.4 0.0 copy-start.1
  1.4 1.4 %copy-done.1 = bf16[3,512,512]{2,1,0:T(8,128)(2,1)S(1)} copy-done((bf16[3,512,512]{2,1,0:T(8,128)(2,1)S(1)}, bf16[3,512,512]{2,1,0:T(8,128)(2,1)}, u32[]{:S(2)}) %copy-start.1) | copy-done | bytes 1572888
  2.8 0.0 copy-start.2
  2.8 1.0 %copy-done.2 = bf16[3,128,512]{2,1,0:T(8,128)(2,1)S(1)} copy-done((bf16[3,128,512]{2,1,0:T(8,128)(2,1)S(1)}, bf16[3,128,512]{2,1,0:T(8,128)(2,1)}, u32[]{:S(2)}) %copy-start.2) | copy-done | bytes 393240
  3.8 0.0 copy-start.3
  3.8 0.7 copy-done.3
  4.5 71.0 %shard_map.46 = bf16[3,128,512]{2,1,0:T(8,128)(2,1)S(1)} custom-call(s32[24]{0:T(128)S(1)} %copy-done.3, bf16[3,128,512]{2,1,0:T(8,128)(2,1)S(1)} %copy-done.2, bf16[3,512,512]{2,1,0:T(8,128)(2,1)S(1)} %copy-done, bf16[3,512,512]{2,1,0:T(8,128)(2,1)S(1)} %copy-done.1), custom_call_target="tpu_custom_call" | custom-call | tf_op jit(solution)/shard_map/pallas_call | solution.py:261
  75.4 0.7 copy.6
Async XLA Ops:
  0.0 1.4 %copy-start = (bf16[3,512,512]{2,1,0:T(8,128)(2,1)S(1)}, bf16[3,512,512]{2,1,0:T(8,128)(2,1)}, u32[]{:S(2)}) copy-start(bf16[3,512,512]{2,1,0:T(8,128)(2,1)} %l_hbm.1) | copy-start | bytes 4718596
  1.4 1.4 %copy-start.1 = (bf16[3,512,512]{2,1,0:T(8,128)(2,1)S(1)}, bf16[3,512,512]{2,1,0:T(8,128)(2,1)}, u32[]{:S(2)}) copy-start(bf16[3,512,512]{2,1,0:T(8,128)(2,1)} %r_hbm.1) | copy-start | bytes 4718596
  2.8 1.0 %copy-start.2 = (bf16[3,128,512]{2,1,0:T(8,128)(2,1)S(1)}, bf16[3,128,512]{2,1,0:T(8,128)(2,1)}, u32[]{:S(2)}) copy-start(bf16[3,128,512]{2,1,0:T(8,128)(2,1)} %g_hbm.1) | copy-start | bytes 1179652
  3.8 0.7 copy-start.3

commit v2 on v1

--- a/solution.py
+++ b/solution.py
@@ -9,6 +9,7 @@
 
 MESH = pl.DeviceIdType.MESH
 CHUNKS = 4
+SPLITS = 1
 
 
 def per_device(gradient, left_factor, right_factor, block_owner):
@@ -81,15 +82,16 @@
 
 
 def preconditioner_kernel(
-    columns, groups, blocks, rows, width, chunks,
+    columns, groups, blocks, rows, width, chunks, splits,
     owner_ref, g_hbm, l_hbm, r_hbm, out_ref,
     gv, lv, rv, snd, gf, lp, pc, rcvc, sely, rcvy, snd2, *rest,
 ):
-    arr = rest[:chunks]
-    res = rest[chunks:2 * chunks]
-    arr2 = rest[2 * chunks:3 * chunks]
+    parts = chunks * splits
+    arr = rest[:parts]
+    res = rest[parts:2 * parts]
+    arr2 = rest[2 * parts:3 * parts]
     (load_sem, fs_s, fs_r, y_s, y_r, c_s, c_r,
-     rc_s, rc_r, ry_s, ry_r, hs_s, hs_r) = rest[3 * chunks:]
+     rc_s, rc_r, ry_s, ry_r, hs_s, hs_r) = rest[3 * parts:]
     col = lax.axis_index("fsdp")
     grp = lax.axis_index("grp")
     core = grp % 2
@@ -97,6 +99,20 @@
     mate = half * 2 + (1 - core)
     across = (1 - half) * 2 + core
     w = width // chunks
+    h = rows // splits
+
+    def cols_of(t):
+        return slice((t // splits) * w, (t // splits + 1) * w)
+
+    def rows_of(t):
+        return pl.ds((t % splits) * h, h)
+
+    def partner(s):
+        d, b = 0, 1
+        while b < columns:
+            v = (col // b) % 2
+            d, b = d + b * ((1 - v) if s & b else v), 2 * b
+        return d
 
     loads = [
         pltpu.make_async_copy(g_hbm, gv, load_sem.at[0]),
@@ -108,7 +124,7 @@
 
     barrier = pltpu.get_barrier_semaphore()
     for s in range(1, columns):
-        pl.semaphore_signal(barrier, inc=1, device_id={"fsdp": (col + s) % columns}, device_id_type=MESH)
+        pl.semaphore_signal(barrier, inc=1, device_id={"fsdp": partner(s)}, device_id_type=MESH)
     pl.semaphore_signal(barrier, inc=1, device_id={"grp": mate}, device_id_type=MESH)
     pl.semaphore_signal(barrier, inc=1, device_id={"grp": across}, device_id_type=MESH)
 
@@ -145,9 +161,8 @@
             k_d = jnp.where(d == s, rank_of[s], k_d)
         return k_d
 
-    order = list(range(1, columns))
-    peers = {s: (col + s) % columns for s in order}
-    senders = {s: (col + columns - s) % columns for s in order}
+    order = list(range(columns - 1, 0, -1))
+    peers = {s: partner(s) for s in order}
 
     def exchange(buf, into, q, s, send_sems, recv_sems):
         return pltpu.make_async_remote_copy(
@@ -158,7 +173,7 @@
 
     def arrival(buf, into, q, s, send_sems, recv_sems):
         return pltpu.make_async_remote_copy(
-            src_ref=buf.at[q, s], dst_ref=into[q].at[senders[s]],
+            src_ref=buf.at[q, s], dst_ref=into[q].at[peers[s]],
             send_sem=send_sems.at[q, s], recv_sem=recv_sems.at[q, s],
             device_id={"fsdp": peers[s]}, device_id_type=MESH,
         )
@@ -172,79 +187,126 @@
     loads[0].wait()
     blocks_to = {s: block_for(peers[s]) for s in order}
     own_block = block_for(col)
-    for q in range(chunks):
-        for s in order:
-            snd[q, s] = gv[blocks_to[s], :, q * w:(q + 1) * w]
-        arr[q][col] = gv[own_block, :, q * w:(q + 1) * w]
+    for t in range(parts):
+        for s in order:
+            snd[t, s] = gv[blocks_to[s], rows_of(t), cols_of(t)]
+        arr[t][col] = gv[own_block, rows_of(t), cols_of(t)]
     pl.semaphore_wait(barrier, columns + 1)
     pending = []
-    for q in range(chunks):
-        for s in order:
-            c = exchange(snd, arr, q, s, fs_s, fs_r)
+    for t in range(parts):
+        for s in order:
+            c = exchange(snd, arr, t, s, fs_s, fs_r)
             c.start()
             pending.append(c)
     loads[1].wait()
     loads[2].wait()
 
-    for q in range(chunks):
-        for s in order:
-            arrival(snd, arr, q, s, fs_s, fs_r).wait_recv()
+    def gathered(t, g):
+        return gf.at[t // splits, g, :, rows_of(t)]
+
+    def across_copy(t, g):
+        return to_group(gathered(t, g), gathered(t, g), y_s.at[t], y_r.at[t], across)
+
+    def mate_copy(t, g, i):
+        return to_group(gathered(t, g), gathered(t, g), c_s.at[t, i], c_r.at[t, i], mate)
+
+    diagonal = (1 - half) * 2 + (1 - core)
+
+    def take_in(t):
+        for s in order:
+            arrival(snd, arr, t, s, fs_s, fs_r).wait_recv()
         for k in range(blocks):
-            gf[q, grp, k] = arr[q][source[k]]
-        first = to_group(gf.at[q, grp], gf.at[q, grp], y_s.at[q], y_r.at[q], across)
+            gf[t // splits, grp, k, rows_of(t)] = arr[t][source[k]]
+        first = across_copy(t, grp)
         first.start()
-        direct = to_group(gf.at[q, grp], gf.at[q, grp], c_s.at[q, 0], c_r.at[q, 0], mate)
+        direct = mate_copy(t, grp, 0)
         direct.start()
-        to_group(gf.at[q, across], gf.at[q, across], y_s.at[q], y_r.at[q], across).wait_recv()
-        onward = to_group(gf.at[q, across], gf.at[q, across], c_s.at[q, 1], c_r.at[q, 1], mate)
+        pending.extend([first, direct])
+
+    def pass_on(t):
+        across_copy(t, across).wait_recv()
+        onward = mate_copy(t, across, 1)
         onward.start()
-        pending += [first, direct, onward]
-        diagonal = (1 - half) * 2 + (1 - core)
-        to_group(gf.at[q, mate], gf.at[q, mate], c_s.at[q, 0], c_r.at[q, 0], mate).wait_recv()
-        to_group(gf.at[q, diagonal], gf.at[q, diagonal], c_s.at[q, 1], c_r.at[q, 1], mate).wait_recv()
+        pending.append(onward)
+
+    def left(q):
+        for t in range(q * splits, (q + 1) * splits):
+            mate_copy(t, mate, 0).wait_recv()
+            mate_copy(t, diagonal, 1).wait_recv()
         for k in range(blocks):
             g_cols = gf[q, :, k].reshape(groups * rows, w)
             lp[k, :, q * w:(q + 1) * w] = jnp.dot(
                 lv[k], g_cols, preferred_element_type=jnp.float32
             ).astype(jnp.bfloat16)
 
-    for q in range(chunks):
+    for t in range(parts):
+        take_in(t)
+        if t > 0:
+            pass_on(t - 1)
+            if t % splits == 0:
+                left(t // splits - 1)
+    pass_on(parts - 1)
+    left(chunks - 1)
+
+    def home_copy(q):
+        return to_group(pc.at[q, 1 - core], rcvc.at[q], rc_s.at[q], rc_r.at[q], mate)
+
+    def right(q):
         for k in range(blocks):
             p = jnp.dot(
                 lp[k], rv[k, :, q * w:(q + 1) * w], preferred_element_type=jnp.float32
             ).astype(jnp.bfloat16)
             for g in range(groups):
                 pc[q, g % 2, g // 2, k] = p[g * rows:(g + 1) * rows]
-        c = to_group(pc.at[q, 1 - core], rcvc.at[q], rc_s.at[q], rc_r.at[q], mate)
+        c = home_copy(q)
         c.start()
         pending.append(c)
 
+    def back_copy(t):
+        return to_group(sely.at[t], rcvy.at[t], ry_s.at[t], ry_r.at[t], across)
+
     def forward_rows(q):
-        to_group(pc.at[q, 1 - core], rcvc.at[q], rc_s.at[q], rc_r.at[q], mate).wait_recv()
-        sely[q] = jnp.where(owner_core == core, pc[q, core, 1 - half], rcvc[q, 1 - half])
-        c = to_group(sely.at[q], rcvy.at[q], ry_s.at[q], ry_r.at[q], across)
-        c.start()
-        return c
-
-    for q in range(chunks):
-        pending.append(forward_rows(q))
+        home_copy(q).wait_recv()
+        for t in range(q * splits, (q + 1) * splits):
+            r = rows_of(t)
+            sely[t] = jnp.where(
+                owner_core == core, pc[q, core, 1 - half, :, r], rcvc[q, 1 - half, :, r]
+            )
+            c = back_copy(t)
+            c.start()
+            pending.append(c)
+
     ranks = {s: rank_for(peers[s]) for s in order}
     own_rank = rank_for(col)
-    for q in range(chunks):
-        to_group(sely.at[q], rcvy.at[q], ry_s.at[q], ry_r.at[q], across).wait_recv()
-        near = jnp.where(owner_core == core, pc[q, core, half], rcvc[q, half])
-        res[q][...] = jnp.where(owner_half == half, near, rcvy[q])
-        for s in order:
-            snd2[q, s] = res[q][ranks[s]]
-            c = exchange(snd2, arr2, q, s, hs_s, hs_r)
+
+    def send_home(t):
+        q, r = t // splits, rows_of(t)
+        back_copy(t).wait_recv()
+        near = jnp.where(owner_core == core, pc[q, core, half, :, r], rcvc[q, half, :, r])
+        res[t][...] = jnp.where(owner_half == half, near, rcvy[t])
+        for s in order:
+            snd2[t, s] = res[t][ranks[s]]
+            c = exchange(snd2, arr2, t, s, hs_s, hs_r)
             c.start()
             pending.append(c)
-        arr2[q][col] = res[q][own_rank]
+        arr2[t][col] = res[t][own_rank]
+
     for q in range(chunks):
-        for s in order:
-            arrival(snd2, arr2, q, s, hs_s, hs_r).wait_recv()
+        right(q)
+        if q > 0:
+            forward_rows(q - 1)
+        if q > 1:
+            send_home((q - 2) * splits)
+    forward_rows(chunks - 1)
+    for t in range(parts):
+        if t % splits or t // splits > chunks - 3:
+            send_home(t)
+
+    for t in range(parts):
+        for s in order:
+            arrival(snd2, arr2, t, s, hs_s, hs_r).wait_recv()
         for j in range(blocks):
-            out_ref[j, :, q * w:(q + 1) * w] = arr2[q][my_dest[j]]
+            out_ref[j, rows_of(t), cols_of(t)] = arr2[t][my_dest[j]]
     for c in pending:
         c.wait_send()
 
@@ -253,13 +315,15 @@
     blocks, rows, width = gradient.shape
     columns = lax.axis_size("fsdp")
     groups = lax.axis_size("grp")
-    q = CHUNKS
+    q, splits = CHUNKS, SPLITS
+    t = q * splits
     w = width // q
+    h = rows // splits
     bf = jnp.bfloat16
     dma = pltpu.SemaphoreType.DMA
-    piece = pltpu.VMEM((columns, rows, w), bf)
+    piece = pltpu.VMEM((columns, h, w), bf)
     return pl.pallas_call(
-        functools.partial(preconditioner_kernel, columns, groups, blocks, rows, width, q),
+        functools.partial(preconditioner_kernel, columns, groups, blocks, rows, width, q, splits),
         out_shape=jax.ShapeDtypeStruct(gradient.shape, gradient.dtype),
         in_specs=[pl.BlockSpec(memory_space=pltpu.SMEM)] + [pl.BlockSpec(memory_space=pl.ANY)] * 3,
         out_specs=pl.BlockSpec(memory_space=pltpu.VMEM),
@@ -267,29 +331,29 @@
             pltpu.VMEM(gradient.shape, bf),
             pltpu.VMEM(left_factor.shape, bf),
             pltpu.VMEM(right_factor.shape, bf),
-            pltpu.VMEM((q, columns, rows, w), bf),
+            pltpu.VMEM((t, columns, h, w), bf),
             pltpu.VMEM((q, groups, blocks, rows, w), bf),
             pltpu.VMEM((blocks, width, width), bf),
             pltpu.VMEM((q, 2, 2, blocks, rows, w), bf),
             pltpu.VMEM((q, 2, blocks, rows, w), bf),
-            pltpu.VMEM((q, blocks, rows, w), bf),
-            pltpu.VMEM((q, blocks, rows, w), bf),
-            pltpu.VMEM((q, columns, rows, w), bf),
+            pltpu.VMEM((t, blocks, h, w), bf),
+            pltpu.VMEM((t, blocks, h, w), bf),
+            pltpu.VMEM((t, columns, h, w), bf),
         ]
-        + [piece] * q
-        + [pltpu.VMEM((blocks, rows, w), bf)] * q
-        + [piece] * q
+        + [piece] * t
+        + [pltpu.VMEM((blocks, h, w), bf)] * t
+        + [piece] * t
         + [
             dma((3,)),
-            dma((q, columns)), dma((q, columns)),
+            dma((t, columns)), dma((t, columns)),
+            dma((t,)), dma((t,)),
+            dma((t, 2)), dma((t, 2)),
             dma((q,)), dma((q,)),
-            dma((q, 2)), dma((q, 2)),
-            dma((q,)), dma((q,)),
-            dma((q,)), dma((q,)),
-            dma((q, columns)), dma((q, columns)),
+            dma((t,)), dma((t,)),
+            dma((t, columns)), dma((t, columns)),
         ],
         compiler_params=pltpu.CompilerParams(
-            collective_id=0, has_side_effects=True, vmem_limit_bytes=48 * 1024 * 1024
+            collective_id=0, has_side_effects=True, vmem_limit_bytes=67043328
         ),
     )(block_owner, gradient, left_factor, right_factor)
 
@@ -299,6 +363,8 @@
     fits = (
         blocks == left_factor.shape[0]
         and lax.axis_size("grp") == 4
+        and lax.axis_size("fsdp") & (lax.axis_size("fsdp") - 1) == 0
+        and gradient.shape[1] % (SPLITS * 16) == 0
         and gradient.shape[2] % (CHUNKS * 128) == 0
     )
     body = per_device_fused if fits else per_device

time: 76.5 us -> 69.3 us (0.906)
  Pallas kernels: 71 us -> 67.4 us
  local copies, waits for them, and re-layouts: 5.21 us -> 1.77 us
    pallas_call x1, Pallas kernels: 71 us -> 67.4 us  [per_device_fused(): pl.pallas_call(functools.partial(preconditioner_kernel, columns, groups,...]
    unnamed x9 -> x1, local copies, waits for them, and re-layouts: 5.21 us -> 1.77 us
where the time goes in v2:
time: 69.3 us; the launch traced here: 69.2 us
  Pallas kernels  67.4 us (97%)
  local copies, waits for them, and re-layouts  1.77 us (3%)
    pallas_call x1, Pallas kernels, per_device_fused(): pl.pallas_call(functools.partial(preconditioner_kernel, columns, groups,...  67.4 us
    unnamed x1, local copies, waits for them, and re-layouts  1.77 us

profile of v2, /device:TPU:0, one launch (start us, length us, event | category | flops | bytes accessed | tf_op | source)
XLA Modules:
  0.0 69.2 jit_solution(476088012310928831)
XLA Ops:
  0.0 67.4 %shard_map.46 = bf16[3,128,512]{2,1,0:T(8,128)(2,1)} custom-call(s32[24]{0:T(128)} %owner_ref.1, bf16[3,128,512]{2,1,0:T(8,128)(2,1)} %g_hbm.1, bf16[3,512,512]{2,1,0:T(8,128)(2,1)} %l_hbm.1, bf16[3,512,512]{2,1,0:T(8,128)(2,1)} %r_hbm.1), custom_call_target="tpu_custom_call" | custom-call | tf_op jit(solution)/shard_map/pallas_call | solution.py:325
  67.4 1.8 %copy.6 = bf16[3,128,512]{2,1,0:T(8,128)(2,1)} copy(bf16[3,128,512]{2,1,0:T(8,128)(2,1)} %shard_map.46) | data formatting | bytes 786432

commit v3 on v0

--- a/solution.py
+++ b/solution.py
@@ -1,7 +1,15 @@
+import functools
+
 import jax
 import jax.numpy as jnp
 from jax import lax
+from jax.experimental import pallas as pl
+from jax.experimental.pallas import tpu as pltpu
 from jax.sharding import PartitionSpec as P
+
+MESH = pl.DeviceIdType.MESH
+CHUNKS = 4
+WINDOW = 2
 
 
 def per_device(gradient, left_factor, right_factor, block_owner):
@@ -73,9 +81,352 @@
     ).astype(jnp.bfloat16)
 
 
+def preconditioner_kernel(
+    columns, groups, blocks, rows, width, chunks, teams,
+    owner_ref, g_hbm, l_hbm, r_hbm, out_ref, gv, lv, rv, load_sem, *rest,
+):
+    rest = list(rest)
+    room = [dict() for _ in teams]
+    for each in room:
+        for name in ("snd", "gf", "lp", "pc", "rcvc", "sely", "rcvy", "snd2"):
+            each[name] = rest.pop(0)
+        for name in ("arr", "res", "arr2"):
+            each[name] = [rest.pop(0) for _ in range(chunks)]
+        for name in ("out", "across", "mate", "home", "back", "ret"):
+            each[name] = (rest.pop(0), rest.pop(0))
+    col = lax.axis_index("fsdp")
+    grp = lax.axis_index("grp")
+    core = grp % 2
+    half = grp // 2
+    mate = half * 2 + (1 - core)
+    across = (1 - half) * 2 + core
+    diagonal = (1 - half) * 2 + (1 - core)
+    w = width // chunks
+
+    def cols_of(q):
+        return slice(q * w, (q + 1) * w)
+
+    def partner(s):
+        d, b = 0, 1
+        while b < columns:
+            v = (col // b) % 2
+            d, b = d + b * ((1 - v) if s & b else v), 2 * b
+        return d
+
+    loads = [
+        pltpu.make_async_copy(g_hbm, gv, load_sem.at[0]),
+        pltpu.make_async_copy(l_hbm, lv, load_sem.at[1]),
+        pltpu.make_async_copy(r_hbm, rv, load_sem.at[2]),
+    ]
+    for load in loads:
+        load.start()
+
+    peers = [partner(s) for s in range(columns)]
+    barrier = pltpu.get_barrier_semaphore()
+    for s in range(1, columns):
+        pl.semaphore_signal(barrier, inc=1, device_id={"fsdp": peers[s]}, device_id_type=MESH)
+    pl.semaphore_signal(barrier, inc=1, device_id={"grp": mate}, device_id_type=MESH)
+    pl.semaphore_signal(barrier, inc=1, device_id={"grp": across}, device_id_type=MESH)
+
+    zero = jnp.int32(0)
+    my_dest = [owner_ref[col * blocks + j] // groups for j in range(blocks)]
+    rank_of = []
+    live_of = []
+    count = zero
+    owner_group = zero
+    for c in range(columns):
+        live = zero
+        for j in range(blocks):
+            o = owner_ref[c * blocks + j]
+            hit = (o // groups) == col
+            live = jnp.where(hit, 1, live)
+            owner_group = jnp.where(hit, o % groups, owner_group)
+        rank_of.append(jnp.minimum(count, blocks - 1))
+        live_of.append(live)
+        count = count + live
+    owner_core = owner_group % 2
+    owner_half = owner_group // 2
+
+    def look_up(table, index):
+        found = zero
+        for n, value in enumerate(table):
+            found = jnp.where(index == n, value, found)
+        return found
+
+    def block_for(d):
+        j_d = zero
+        for j in range(1, blocks):
+            j_d = jnp.where(my_dest[j] == d, j, j_d)
+        return j_d
+
+    plan = []
+    for team, each in zip(teams, room):
+        size = min(blocks, len(team))
+        entry = [zero] * size
+        slot = [zero] * size
+        place = []
+        filled = zero
+        for i, s in enumerate(team):
+            live = look_up(live_of, peers[s])
+            rank = look_up(rank_of, peers[s])
+            for p in range(size):
+                take = (live == 1) & (filled == p)
+                entry[p] = jnp.where(take, i, entry[p])
+                slot[p] = jnp.where(take, rank, slot[p])
+            place.append(jnp.minimum(filled, size - 1))
+            filled = filled + live
+        at_home = []
+        for j in range(blocks):
+            inside, index = zero, zero
+            for i, s in enumerate(team):
+                hit = my_dest[j] == peers[s]
+                inside = jnp.where(hit, 1, inside)
+                index = jnp.where(hit, i, index)
+            at_home.append((inside, index))
+        plan.append((size, entry, slot, place, at_home))
+
+    pending = []
+
+    def launch(copy):
+        copy.start()
+        pending.append(copy)
+
+    def exchange(a, src, dst, way, q, i):
+        sems = room[a][way]
+        return pltpu.make_async_remote_copy(
+            src_ref=room[a][src].at[q, i], dst_ref=room[a][dst][q].at[i],
+            send_sem=sems[0].at[q, i], recv_sem=sems[1].at[q, i],
+            device_id={"fsdp": peers[teams[a][i]]}, device_id_type=MESH,
+        )
+
+    def to_group(src, dst, sems, index, g):
+        return pltpu.make_async_remote_copy(
+            src_ref=src, dst_ref=dst,
+            send_sem=sems[0].at[index], recv_sem=sems[1].at[index],
+            device_id={"grp": g}, device_id_type=MESH,
+        )
+
+    def across_copy(a, q, g):
+        piece = room[a]["gf"].at[q, g]
+        return to_group(piece, piece, room[a]["across"], (q,), across)
+
+    def mate_copy(a, q, g, i):
+        piece = room[a]["gf"].at[q, g]
+        return to_group(piece, piece, room[a]["mate"], (q, i), mate)
+
+    def home_copy(a, q):
+        return to_group(
+            room[a]["pc"].at[q, 1 - core], room[a]["rcvc"].at[q], room[a]["home"], (q,), mate
+        )
+
+    def back_copy(a, q):
+        return to_group(room[a]["sely"].at[q], room[a]["rcvy"].at[q], room[a]["back"], (q,), across)
+
+    def pack(a, q):
+        for i, s in enumerate(teams[a]):
+            piece = gv[block_for(peers[s]), :, cols_of(q)]
+            if s:
+                room[a]["snd"][q, i] = piece
+            else:
+                room[a]["arr"][q][i] = piece
+
+    def send_out(a, q):
+        for i, s in enumerate(teams[a]):
+            if s:
+                launch(exchange(a, "snd", "arr", "out", q, i))
+
+    def take_in(a, q):
+        for i, s in enumerate(teams[a]):
+            if s:
+                exchange(a, "snd", "arr", "out", q, i).wait_recv()
+        for b, r in queue[a * chunks + q + WINDOW:a * chunks + q + WINDOW + 1]:
+            send_out(b, r)
+        size, entry = plan[a][:2]
+        for p in range(size):
+            room[a]["gf"][q, grp, p] = room[a]["arr"][q][entry[p]]
+        launch(across_copy(a, q, grp))
+        launch(mate_copy(a, q, grp, 0))
+
+    def pass_on(a, q):
+        across_copy(a, q, across).wait_recv()
+        launch(mate_copy(a, q, across, 1))
+
+    def left(a, q):
+        mate_copy(a, q, mate, 0).wait_recv()
+        mate_copy(a, q, diagonal, 1).wait_recv()
+        size, _, slot = plan[a][:3]
+        for p in range(size):
+            g_cols = room[a]["gf"][q, :, p].reshape(groups * rows, w)
+            room[a]["lp"][p, :, cols_of(q)] = jnp.dot(
+                lv[slot[p]], g_cols, preferred_element_type=jnp.float32
+            ).astype(jnp.bfloat16)
+
+    def right(a, q):
+        size, _, slot = plan[a][:3]
+        for p in range(size):
+            product = jnp.dot(
+                room[a]["lp"][p], rv[slot[p], :, cols_of(q)], preferred_element_type=jnp.float32
+            ).astype(jnp.bfloat16)
+            for g in range(groups):
+                room[a]["pc"][q, g % 2, g // 2, p] = product[g * rows:(g + 1) * rows]
+        launch(home_copy(a, q))
+
+    def owner_side(a, q, which):
+        return jnp.where(owner_core == core, room[a]["pc"][q, core, which], room[a]["rcvc"][q, which])
+
+    def forward_rows(a, q):
+        home_copy(a, q).wait_recv()
+        room[a]["sely"][q] = owner_side(a, q, 1 - half)
+        launch(back_copy(a, q))
+
+    def send_home(a, q):
+        back_copy(a, q).wait_recv()
+        res = room[a]["res"][q]
+        res[...] = jnp.where(owner_half == half, owner_side(a, q, half), room[a]["rcvy"][q])
+        place = plan[a][3]
+        for i, s in enumerate(teams[a]):
+            if s:
+                room[a]["snd2"][q, i] = res[place[i]]
+                launch(exchange(a, "snd2", "arr2", "ret", q, i))
+            else:
+                room[a]["arr2"][q][i] = res[place[i]]
+
+    loads[0].wait()
+    for q in range(chunks):
+        pack(0, q)
+    pl.semaphore_wait(barrier, columns + 1)
+    queue = [(a, q) for a in range(len(teams)) for q in range(chunks)]
+    for a, q in queue[:WINDOW]:
+        send_out(a, q)
+    for q in range(chunks):
+        pack(1, q)
+    loads[1].wait()
+    loads[2].wait()
+
+    last = chunks - 1
+    def take_back(a, q):
+        for i, s in enumerate(teams[a]):
+            if s:
+                exchange(a, "snd2", "arr2", "ret", q, i).wait_recv()
+
+    def take_in_next(a, q):
+        take_in(a, q)
+        if q > 0:
+            pass_on(a, q - 1)
+            left(a, q - 1)
+
+    def finish(a):
+        pass_on(a, last)
+        left(a, last)
+
+    def rights(a, start, stop):
+        for q in range(start, stop):
+            right(a, q)
+            if q > 0:
+                forward_rows(a, q - 1)
+        if stop == chunks:
+            forward_rows(a, last)
+
+    for q in range(chunks):
+        take_in_next(0, q)
+    finish(0)
+    middle = chunks // 2
+    take_in_next(1, 0)
+    rights(0, 0, middle)
+    for q in range(1, chunks):
+        take_in_next(1, q)
+        if q == 1:
+            rights(0, middle, chunks)
+        if q >= chunks - 2:
+            send_home(0, q - (chunks - 2))
+    finish(1)
+    right(1, 0)
+    for q in range(2, chunks):
+        take_back(0, q - 2)
+        send_home(0, q)
+        rights(1, q - 1, q)
+    rights(1, chunks - 1, chunks)
+    for q in range(chunks):
+        take_back(*((0, chunks - 2 + q) if q < 2 else (1, q - 2)))
+        send_home(1, q)
+    take_back(1, chunks - 2)
+    take_back(1, last)
+
+    for q in range(chunks):
+        for j in range(blocks):
+            inside, index = plan[0][4][j]
+            out_ref[j, :, cols_of(q)] = jnp.where(
+                inside == 1, room[0]["arr2"][q][index], room[1]["arr2"][q][plan[1][4][j][1]]
+            )
+    for copy in pending:
+        copy.wait_send()
+
+
+def per_device_fused(gradient, left_factor, right_factor, block_owner):
+    blocks, rows, width = gradient.shape
+    columns = lax.axis_size("fsdp")
+    groups = lax.axis_size("grp")
+    q = CHUNKS
+    w = width // q
+    bf = gradient.dtype
+    dma = pltpu.SemaphoreType.DMA
+    early = list(range(columns // 2, columns // 2 + columns // 4))
+    late = [s for s in range(columns - 1, -1, -1) if s not in early]
+    teams = (early, late)
+    scratch = [
+        pltpu.VMEM(gradient.shape, bf),
+        pltpu.VMEM(left_factor.shape, bf),
+        pltpu.VMEM(right_factor.shape, bf),
+        dma((3,)),
+    ]
+    for team in teams:
+        n, m = len(team), min(blocks, len(team))
+        scratch += [
+            pltpu.VMEM((q, n, rows, w), bf),
+            pltpu.VMEM((q, groups, m, rows, w), bf),
+            pltpu.VMEM((m, width, width), bf),
+            pltpu.VMEM((q, 2, 2, m, rows, w), bf),
+            pltpu.VMEM((q, 2, m, rows, w), bf),
+            pltpu.VMEM((q, m, rows, w), bf),
+            pltpu.VMEM((q, m, rows, w), bf),
+            pltpu.VMEM((q, n, rows, w), bf),
+        ]
+        scratch += [pltpu.VMEM((n, rows, w), bf)] * q
+        scratch += [pltpu.VMEM((m, rows, w), bf)] * q
+        scratch += [pltpu.VMEM((n, rows, w), bf)] * q
+        for shape in ((q, n), (q,), (q, 2), (q,), (q,), (q, n)):
+            scratch += [dma(shape), dma(shape)]
+    return pl.pallas_call(
+        functools.partial(
+            preconditioner_kernel, columns, groups, blocks, rows, width, q, teams
+        ),
+        out_shape=jax.ShapeDtypeStruct(gradient.shape, gradient.dtype),
+        in_specs=[pl.BlockSpec(memory_space=pltpu.SMEM)] + [pl.BlockSpec(memory_space=pl.ANY)] * 3,
+        out_specs=pl.BlockSpec(memory_space=pltpu.VMEM),
+        scratch_shapes=scratch,
+        compiler_params=pltpu.CompilerParams(
+            collective_id=0, has_side_effects=True, vmem_limit_bytes=67043328
+        ),
+    )(block_owner, gradient, left_factor, right_factor)
+
+
+def per_device_any(gradient, left_factor, right_factor, block_owner):
+    blocks = gradient.shape[0]
+    columns = lax.axis_size("fsdp")
+    fits = (
+        blocks == left_factor.shape[0]
+        and lax.axis_size("grp") == 4
+        and columns >= 4
+        and columns & (columns - 1) == 0
+        and gradient.shape[2] % (CHUNKS * 128) == 0
+    )
+    body = per_device_fused if fits else per_device
+    return body(gradient, left_factor, right_factor, block_owner)
+
+
 def solution(mesh):
     return jax.shard_map(
-        per_device,
+        per_device_any,
         mesh=mesh,
         in_specs=(
             P("fsdp", "grp", None),

time: 136 us -> 69.1 us (0.51)
  blocking collectives: 85.9 us -> 0 us
  Pallas kernels: 0 us -> 67.1 us
  waiting for transfers between devices: 25.4 us -> 0 us
  matrix products: 9.85 us -> 0 us
  starting transfers between devices: 7.28 us -> 0 us
  local copies, waits for them, and re-layouts: 6.34 us -> 1.77 us
    all_to_all x3 -> x0, blocking collectives: 85.9 us -> none  [the longest x1 28.9 us: per_device(): lax.all_to_all(packed, 'grp', split_axis=1, concat_axis=1, tiled=True)]
    pallas_call x0 -> x1, Pallas kernels: none -> 67.1 us  [per_device_fused(): pl.pallas_call(functools.partial(preconditioner_kernel, columns, groups,...]
    all_to_all x1 -> x0, waiting for transfers between devices: 25.4 us -> none  [per_device(): lax.all_to_all(outgoing.reshape(columns * piece_rows, block_width), 'fsdp...]
    dot_general x5 -> x0, matrix products: 9.85 us -> none  [the longest x1 4.21 us: per_device(): jnp.einsum('kab,kbc->kac', left_product, right_factor, preferred_element_...]
    all_to_all x1 -> x0, starting transfers between devices: 7.28 us -> none  [per_device(): lax.all_to_all(outgoing.reshape(columns * piece_rows, block_width), 'fsdp...]
    convert_element_type x5 -> x0, local copies, waits for them, and re-layouts: 4.12 us -> none  [the longest x1 1.35 us: per_device(): result = jnp.einsum('kab,kbc->kac', left_product, right_factor, preferred...]
    reshape x2 -> x0, local copies, waits for them, and re-layouts: 2.2 us -> none  [the longest x1 1.35 us: per_device(): packed = packed.reshape(slot_count, groups * piece_rows, block_width)]
    unnamed x2 -> x1, local copies, waits for them, and re-layouts: 0.01 us -> 1.77 us
  transfers between devices with their start and end apart: 1 -> 0, of which waited for: 1 -> 0; matrix products, arithmetic and copies ran while one was open for 0% -> 0% of each run, Pallas kernels for 0% -> 0%
where the time goes in v3:
time: 69.1 us; the launch traced here: 68.9 us
  Pallas kernels  67.1 us (97%)
  local copies, waits for them, and re-layouts  1.77 us (3%)
    pallas_call x1, Pallas kernels, per_device_fused(): pl.pallas_call(functools.partial(preconditioner_kernel, columns, groups,...  67.1 us
    unnamed x1, local copies, waits for them, and re-layouts  1.77 us

profile of v3, /device:TPU:0, one launch (start us, length us, event | category | flops | bytes accessed | tf_op | source)
XLA Modules:
  0.0 68.9 jit_solution(15484717189602647539)
XLA Ops:
  0.0 67.1 %shard_map.46 = bf16[3,128,512]{2,1,0:T(8,128)(2,1)} custom-call(s32[24]{0:T(128)} %owner_ref.1, bf16[3,128,512]{2,1,0:T(8,128)(2,1)} %g_hbm.1, bf16[3,512,512]{2,1,0:T(8,128)(2,1)} %l_hbm.1, bf16[3,512,512]{2,1,0:T(8,128)(2,1)} %r_hbm.1), custom_call_target="tpu_custom_call" | custom-call | tf_op jit(solution)/shard_map/pallas_call | solution.py:399
  67.1 1.8 %copy.6 = bf16[3,128,512]{2,1,0:T(8,128)(2,1)} copy(bf16[3,128,512]{2,1,0:T(8,128)(2,1)} %shard_map.46) | data formatting | bytes 786432

commit v4 on v3

--- a/solution.py
+++ b/solution.py
@@ -370,7 +370,7 @@
     w = width // q
     bf = gradient.dtype
     dma = pltpu.SemaphoreType.DMA
-    early = list(range(columns // 2, columns // 2 + columns // 4))
+    early = [columns // 2, columns - 1]
     late = [s for s in range(columns - 1, -1, -1) if s not in early]
     teams = (early, late)
     scratch = [

time: 69.1 us -> 69.3 us (level)
  no operation moved by 1% of the time
where the time goes in v4:
time: 69.3 us; the launch traced here: 69.1 us
  Pallas kernels  67.4 us (97%)
  local copies, waits for them, and re-layouts  1.77 us (3%)
    pallas_call x1, Pallas kernels, per_device_fused(): pl.pallas_call(functools.partial(preconditioner_kernel, columns, groups,...  67.4 us
    unnamed x1, local copies, waits for them, and re-layouts  1.77 us

profile of v4, /device:TPU:0, one launch (start us, length us, event | category | flops | bytes accessed | tf_op | source)
XLA Modules:
  0.0 69.1 jit_solution(13697201483743143437)
XLA Ops:
  0.0 67.4 %shard_map.46 = bf16[3,128,512]{2,1,0:T(8,128)(2,1)} custom-call(s32[24]{0:T(128)} %owner_ref.1, bf16[3,128,512]{2,1,0:T(8,128)(2,1)} %g_hbm.1, bf16[3,512,512]{2,1,0:T(8,128)(2,1)} %l_hbm.1, bf16[3,512,512]{2,1,0:T(8,128)(2,1)} %r_hbm.1), custom_call_target="tpu_custom_call" | custom-call | tf_op jit(solution)/shard_map/pallas_call | solution.py:399
  67.4 1.8 %copy.6 = bf16[3,128,512]{2,1,0:T(8,128)(2,1)} copy(bf16[3,128,512]{2,1,0:T(8,128)(2,1)} %shard_map.46) | data formatting | bytes 786432
